TPU v7x, 32 devices: a whole 2x2x4 slice. The times are simulated.
32 devices in a mesh: row: 8 (over y, x, core), depth: 4 (over z).
Axes of the slice: x: 2, y: 2, z: 4, core: 2. Of those that a mesh axis runs over, the one named last changes fastest.
Arguments:
- l_cores: float32 [16, 32, 384, 384], P('row', 'depth'), may hold values from -0.0546875 to 0.0546875
- l_bucket: int32 [16, 32], P('row', 'depth'), may hold values from 1 to 3
- present: int32 [16, 32], P('row', 'depth'), may hold values 0 or 1
- u_cores: float32 [32, 4, 384, 384], P('depth', None, 'row'), may hold values from -6 to 6
- u_bucket: int32 [32, 4], P('depth'), may hold values from 1 to 3
- diag_cores: float32 [16, 4, 384, 384], P('row', None, 'depth'), may hold values from -6 to 6
- pivot_inv: float32 [4, 384, 384], P(None, 'row'), may hold values from -0.3125 to 0.3125
- coupling: float32 [3, 384, 384], P(None, 'row'), may hold values from -0.21875 to 0.21875
Outputs:
- finished: float32 [16, 4, 384, 384], P('row', None, 'depth')
Inputs may be any that keep to these rules, and one draw needn't show every extreme that they name: A lower tile's core rank is l_bucket * 128. An upper tile's core rank is u_bucket * 128. `present`: 1 marks a nonzero lower tile.
All inputs are finite; a program needn't handle non-finite values. No bound on the sum of `present` on one device may be relied on, other than what follows from the above.
Results may differ from a plain program's by a relative error of at most 0.0003.
Values sent between devices are 32-bit elements; how exact they have to be, the bound alone decides.
No kernel may reach another device: no remote copies, remote signals or barrier semaphores. Data moves between devices by JAX's collectives and lax.ppermute only.
A program may use at most 128 MiB of HBM per device.

v0:
```python
import jax
import jax.numpy as jnp
from jax import lax
from jax.sharding import PartitionSpec as P

HIGH = lax.Precision.HIGHEST


def per_device(l_cores, l_bucket, present, u_cores, u_bucket, diag_cores, pivot_inv, coupling):
    width = l_cores.shape[-1]
    rank_step = width // 3
    share_rows = diag_cores.shape[2]
    pivots, links = (
        lax.all_gather(pivot_inv, "row", axis=1, tiled=True),
        lax.all_gather(coupling, "row", axis=1, tiled=True),
    )
    positions = jnp.arange(width, dtype=jnp.int32)
    col_keep = (
        (positions[None, None, :] < (l_bucket * rank_step)[:, :, None]) & (present[:, :, None] > 0)
    ).astype(jnp.float32)
    l_masked = l_cores * col_keep[:, :, None, :]
    u_limits = u_bucket * rank_step
    portion = lax.all_gather(u_cores, "row", axis=2, tiled=True)
    count_rows = portion.shape[2]
    row_ids = jnp.arange(count_rows, dtype=jnp.int32)
    row_mask = (row_ids[None, None, :] < u_limits[:, :, None]).astype(jnp.float32)
    u_masked = portion * row_mask[..., None]
    partial_update = jnp.einsum("ikar,kjrb->ijab", l_masked, u_masked, precision=HIGH)
    summed = lax.psum(partial_update, "depth")
    own_rows = lax.dynamic_slice_in_dim(summed, lax.axis_index("depth") * share_rows, share_rows, 2)
    reduced = diag_cores - own_rows
    previous = jnp.einsum("iab,bc->iac", reduced[:, 0], pivots[0], precision=HIGH)
    results = [previous]
    for column in range(1, reduced.shape[1]):
        linked = jnp.einsum("iab,bc->iac", previous, links[column - 1], precision=HIGH)
        previous = jnp.einsum(
            "iab,bc->iac", reduced[:, column] - linked, pivots[column], precision=HIGH
        )
        results.append(previous)
    return jnp.stack(results, axis=1)


def solution(mesh):
    in_specs = (
        P("row", "depth", None, None),
        P("row", "depth"),
        P("row", "depth"),
        P("depth", None, "row", None),
        P("depth", None),
        P("row", None, "depth", None),
        P(None, "row", None),
        P(None, "row", None),
    )
    out_specs = P("row", None, "depth", None)
    return jax.shard_map(
        per_device, mesh=mesh, in_specs=in_specs, out_specs=out_specs, check_vma=False
    )
```

profile of v0, /device:TPU:0, one launch (start us, length us, event | category | flops | bytes accessed | tf_op | source)
XLA Modules:
  0.0 453.8 jit_solution(7917406552698786464)
XLA Ops:
  6.5 0.7 all-gather.4.cloned.1.call-update
  7.3 0.1 copy.9
  7.4 0.1 fusion.15
  7.5 0.1 fusion.13
  7.6 103.0 %all-gather.4.cloned.1.call-done = f32[8,4,384,384]{3,2,1,0:T(8,128)} async-done(((f32[8,4,48,384]{3,2,1,0:T(8,128)}), f32[8,4,384,384]{3,2,1,0:T(8,128)}) %all-gather.4.cloned.1.call-update) | async-done | bytes 18874384 | tf_op jit(solution)/shard_map/all_gather | solution.py:23
  110.6 94.9 %fusion.5 = f32[2,4,384,384]{2,3,0,1:T(8,128)} fusion(f32[2,8,384,384]{3,2,1,0:T(8,128)} %param.8, f32[2,8,384]{2,1,0:T(8,128)S(1)} %fusion.15, f32[8,4,384,384]{3,2,1,0:T(8,128)} %all-gather.4.cloned.1.call-done, f32[8,4,384]{2,1,0:T(4,128)S(1)} %fusion.13), kind=kOutput, calls=%fused_computation.6 | convolution fusion | flops 43493621760 | bytes 33103872 | tf_op jit(solution)/shard_map/ikar,kjrb->ijab/dot_general | solution.py:28
  205.5 0.0 all-gather.6.cloned.1.call-start
  205.6 0.7 all-gather.6.cloned.1.call-update
  206.3 0.0 all-gather.8.cloned.1.call-start
  206.3 0.5 all-gather.8.cloned.1.call-update
  206.9 0.5 copy.11
  207.3 170.3 %all-reduce.2.cloned.1.call-done = f32[2,4,384,384]{2,3,0,1:T(8,128)} async-done(((f32[2,4,384,384]{2,3,0,1:T(8,128)}), f32[2,4,384,384]{2,3,0,1:T(8,128)}) %all-reduce.2.cloned.1.call-update) | async-done | bytes 4718608 | tf_op jit(solution)/shard_map/psum | solution.py:29
  377.6 2.4 dynamic-slice_subtract_fusion
  380.0 27.4 %all-gather.6.cloned.1.call-done = f32[4,384,384]{2,1,0:T(8,128)} async-done(((f32[4,48,384]{2,1,0:T(8,128)}), f32[4,384,384]{2,1,0:T(8,128)}) %all-gather.6.cloned.1.call-update) | async-done | bytes 2359312 | tf_op jit(solution)/shard_map/all_gather | solution.py:14
  407.4 1.9 fusion.12
  409.4 26.3 %all-gather.8.cloned.1.call-done = f32[3,384,384]{2,1,0:T(8,128)} async-done(((f32[3,48,384]{2,1,0:T(8,128)}), f32[3,384,384]{2,1,0:T(8,128)}) %all-gather.8.cloned.1.call-update) | async-done | bytes 1769488 | tf_op jit(solution)/shard_map/all_gather | solution.py:15
  435.6 2.3 convolution_subtract_fusion.2
  437.9 2.0 fusion.11
  439.9 2.2 convolution_subtract_fusion.1
  442.1 0.9 fusion.10
  443.0 2.2 convolution_subtract_fusion
  445.2 0.9 convolution_bitcast_fusion
  446.1 0.1 pad_maximum_fusion
  446.2 1.1 copy.16
  (16 shorter events, 0.1 us)
Async XLA Ops:
  6.5 0.8 copy-start.2
  6.5 0.9 copy-start.4
  6.5 0.9 copy-start.3
  6.5 104.1 %all-gather.4.cloned.1.call-start = ((), (), s32[]{:S(2)}) async-start(), calls=%async_computation | async-start | bytes 21233664 | tf_op jit(solution)/shard_map/all_gather | solution.py:23
  7.3 370.4 %all-reduce.2.cloned.1.call-start = ((), (), s32[]{:S(2)}) async-start(), calls=%async_computation.1 | async-start | bytes 9437184 | tf_op jit(solution)/shard_map/psum | solution.py:29
  205.5 1.3 copy-start.1
  205.5 201.9 %all-gather.6.cloned.1.call-start = ((), (), s32[]{:S(2)}) async-start(), calls=%async_computation.2 | async-start | bytes 2654208 | tf_op jit(solution)/shard_map/all_gather | solution.py:14
  206.3 229.3 %all-gather.8.cloned.1.call-start = ((), (), s32[]{:S(2)}) async-start(), calls=%async_computation.3 | async-start | bytes 1990656 | tf_op jit(solution)/shard_map/all_gather | solution.py:15
  435.6 6.5 %copy-start = (f32[4,384,384]{2,1,0:T(8,128)S(1)}, f32[4,384,384]{2,1,0:T(8,128)}, u32[]{:S(2)}) copy-start(f32[4,384,384]{2,1,0:T(8,128)} %all-gather.6.cloned.1.call-done) | copy-start | bytes 7077892
Sparse Core Ops, SparseCore 0:
  9.2 101.3 all-gather.3
  205.7 171.9 all-reduce.1
  379.5 27.8 all-gather.5
  409.2 26.3 all-gather.7
where the time goes:
time: 454 us
  waiting for transfers between devices  329 us (72%)
  matrix products  107 us (24%)
  between operations  13.3 us (3%)
    psum x1, waiting for transfers between devices, per_device(): summed = lax.psum(partial_update, 'depth')  170 us
    all_gather x1, waiting for transfers between devices, per_device(): portion = lax.all_gather(u_cores, 'row', axis=2, tiled=True)  103 us
    dot_general x1, matrix products, per_device(): jnp.einsum('ikar,kjrb->ijab', l_masked, u_masked, precision=HIGH)  94.9 us
    all_gather x1, waiting for transfers between devices, per_device(): lax.all_gather(pivot_inv, 'row', axis=1, tiled=True)  27.4 us
    all_gather x1, waiting for transfers between devices, per_device(): lax.all_gather(coupling, 'row', axis=1, tiled=True)  26.3 us
  transfers between devices with their start and end apart: 4, of which 4 were waited for; matrix products, arithmetic and copies ran while one was open for 1% of the time, Pallas kernels for 0%

commit v1 on v0

--- a/solution.py
+++ b/solution.py
@@ -6,12 +6,17 @@
 HIGH = lax.Precision.HIGHEST
 
 
+def stack_and_merge(value, axis, dim):
+    parts = lax.all_gather(value, axis)
+    return jnp.concatenate(parts, axis=dim)
+
+
 def per_device(l_cores, l_bucket, present, u_cores, u_bucket, diag_cores, pivot_inv, coupling):
     width = l_cores.shape[-1]
     rank_step = width // 3
     share_rows = diag_cores.shape[2]
     pivots, links = (
-        lax.all_gather(pivot_inv, "row", axis=1, tiled=True),
+        stack_and_merge(pivot_inv, "row", 1),
         lax.all_gather(coupling, "row", axis=1, tiled=True),
     )
     positions = jnp.arange(width, dtype=jnp.int32)

time: 454 us -> 420 us (0.925)
  waiting for transfers between devices: 329 us -> 295 us
    all_gather x1, waiting for transfers between devices: 27.4 us -> 0.02 us  [stack_and_merge(): parts = lax.all_gather(value, axis)]
  transfers between devices with their start and end apart: 4 -> 4, of which waited for: 4 -> 3; matrix products, arithmetic and copies ran while one was open for 1% -> 24% of each run, Pallas kernels for 0% -> 0%
where the time goes in v1:
time: 420 us
  waiting for transfers between devices  295 us (70%)
  matrix products  103 us (25%)
  between operations  13.3 us (3%)
  local copies, waits for them, and re-layouts  5.66 us (1%)
    psum x1, waiting for transfers between devices, per_device(): summed = lax.psum(partial_update, 'depth')  167 us
    all_gather x1, waiting for transfers between devices, per_device(): portion = lax.all_gather(u_cores, 'row', axis=2, tiled=True)  102 us
    dot_general x1, matrix products, per_device(): jnp.einsum('ikar,kjrb->ijab', l_masked, u_masked, precision=HIGH)  94.9 us
    all_gather x1, waiting for transfers between devices, per_device(): lax.all_gather(coupling, 'row', axis=1, tiled=True)  23.8 us
  transfers between devices with their start and end apart: 4, of which 3 were waited for; matrix products, arithmetic and copies ran while one was open for 24% of the time, Pallas kernels for 0%

profile of v1, /device:TPU:0, one launch (start us, length us, event | category | flops | bytes accessed | tf_op | source)
XLA Modules:
  0.0 419.8 jit_solution(15169069880974969929)
XLA Ops:
  6.5 0.7 all-gather.5.cloned.1.call-update
  7.3 0.7 all-gather.9.cloned.1.call-update
  8.1 0.1 copy.18
  8.2 0.1 fusion.13
  8.3 0.1 fusion.11
  8.3 102.3 %all-gather.5.cloned.1.call-done = f32[8,4,384,384]{3,2,1,0:T(8,128)} async-done(((f32[8,4,48,384]{3,2,1,0:T(8,128)}), f32[8,4,384,384]{3,2,1,0:T(8,128)}) %all-gather.5.cloned.1.call-update) | async-done | bytes 18874384 | tf_op jit(solution)/shard_map/all_gather | solution.py:28
  110.6 94.9 %fusion.5 = f32[2,4,384,384]{2,3,0,1:T(8,128)} fusion(f32[2,8,384,384]{3,2,1,0:T(8,128)} %param.8, f32[2,8,384]{2,1,0:T(8,128)S(1)} %fusion.13, f32[8,4,384,384]{3,2,1,0:T(8,128)} %all-gather.5.cloned.1.call-done, f32[8,4,384]{2,1,0:T(4,128)S(1)} %fusion.11), kind=kOutput, calls=%fused_computation.7 | convolution fusion | flops 43493621760 | bytes 33103872 | tf_op jit(solution)/shard_map/ikar,kjrb->ijab/dot_general | solution.py:33
  205.6 0.5 all-gather.7.cloned.1.call-update
  206.1 0.7 copy-done.5
  206.8 0.5 copy.20
  207.3 1.8 copy.43
  209.1 1.5 fusion.14
  210.6 167.0 %all-reduce.2.cloned.1.call-done = f32[2,4,384,384]{2,3,0,1:T(8,128)} async-done(((f32[2,4,384,384]{2,3,0,1:T(8,128)}), f32[2,4,384,384]{2,3,0,1:T(8,128)}) %all-reduce.2.cloned.1.call-update) | async-done | bytes 4718608 | tf_op jit(solution)/shard_map/psum | solution.py:34
  377.6 2.4 dynamic-slice_subtract_fusion
  380.1 0.9 fusion.10
  381.0 23.8 %all-gather.7.cloned.1.call-done = f32[3,384,384]{2,1,0:T(8,128)} async-done(((f32[3,48,384]{2,1,0:T(8,128)}), f32[3,384,384]{2,1,0:T(8,128)}) %all-gather.7.cloned.1.call-update) | async-done | bytes 1769488 | tf_op jit(solution)/shard_map/all_gather | solution.py:20
  404.8 2.3 convolution_subtract_fusion.2
  407.1 0.9 fusion.15
  408.0 1.1 convolution_subtract_fusion.1
  409.2 0.9 fusion.16
  410.1 1.1 convolution_subtract_fusion
  411.2 0.9 convolution_bitcast_fusion
  412.1 0.1 pad_maximum_fusion
  412.2 1.1 copy.26
  (26 shorter events, 0.2 us)
Async XLA Ops:
  6.5 1.5 copy-start.6
  6.5 1.6 copy-start.8
  6.5 1.6 copy-start.7
  6.5 104.1 %all-gather.5.cloned.1.call-start = ((), (), s32[]{:S(2)}) async-start(), calls=%async_computation | async-start | bytes 21233664 | tf_op jit(solution)/shard_map/all_gather | solution.py:28
  7.3 200.0 %all-gather.9.cloned.1.call-start = ((), (), s32[]{:S(2)}) async-start(), calls=%async_computation.3 | async-start | bytes 2654208 | tf_op jit(solution)/shard_map/all_gather | solution.py:10
  8.0 369.6 %all-reduce.2.cloned.1.call-start = ((), (), s32[]{:S(2)}) async-start(), calls=%async_computation.1 | async-start | bytes 9437184 | tf_op jit(solution)/shard_map/psum | solution.py:34
  205.5 1.3 copy-start.5
  205.5 199.3 %all-gather.7.cloned.1.call-start = ((), (), s32[]{:S(2)}) async-start(), calls=%async_computation.2 | async-start | bytes 1990656 | tf_op jit(solution)/shard_map/all_gather | solution.py:20
  377.6 2.4 copy-start.3
  380.1 27.0 %copy-start.2 = (f32[1,8,48,384]{3,2,1,0:T(8,128)S(1)}, f32[1,8,48,384]{3,2,1,0:T(8,128)}, u32[]{:S(2)}) copy-start(f32[1,8,48,384]{3,2,1,0:T(8,128)} %get-tuple-element.7) | copy-start | bytes 1769476
  404.8 3.3 copy-start.4
  407.1 2.1 copy-start.1
  409.2 2.1 copy-start
Sparse Core Ops, SparseCore 0:
  9.2 101.3 all-gather.4
  112.5 28.8 all-gather.8
  205.7 171.9 all-reduce.1
  379.4 25.3 all-gather.6

commit v2 on v0

--- a/solution.py
+++ b/solution.py
@@ -1,9 +1,26 @@
+import functools
 import jax
 import jax.numpy as jnp
 from jax import lax
 from jax.sharding import PartitionSpec as P
 
 HIGH = lax.Precision.HIGHEST
+
+
+def draw_packet(here_x, mesh_ax):
+    n_all = lax.psum(1, mesh_ax)
+    u_next, prior = (here_x, 0)
+    while 1 << prior < n_all:
+        rows = []
+        for idx in [*range(n_all)]:
+            rows.append((idx, idx ^ 1 << prior))
+        long_array = lax.ppermute(u_next, mesh_ax, rows)
+        u_next = u_next + long_array
+        prior = prior + 1
+    return u_next
+
+
+bind_the_tokens = functools.partial(draw_packet, mesh_ax="depth")
 
 
 def per_device(l_cores, l_bucket, present, u_cores, u_bucket, diag_cores, pivot_inv, coupling):
@@ -26,7 +43,7 @@
     row_mask = (row_ids[None, None, :] < u_limits[:, :, None]).astype(jnp.float32)
     u_masked = portion * row_mask[..., None]
     partial_update = jnp.einsum("ikar,kjrb->ijab", l_masked, u_masked, precision=HIGH)
-    summed = lax.psum(partial_update, "depth")
+    summed = bind_the_tokens(partial_update)
     own_rows = lax.dynamic_slice_in_dim(summed, lax.axis_index("depth") * share_rows, share_rows, 2)
     reduced = diag_cores - own_rows
     previous = jnp.einsum("iab,bc->iac", reduced[:, 0], pivots[0], precision=HIGH)

time: 454 us -> 502 us (1.11)
  waiting for transfers between devices: 329 us -> 409 us
  matrix products: 107 us -> 64.9 us
  other arithmetic: 2.6 us -> 8.49 us
    ppermute x0 -> x2, waiting for transfers between devices: none -> 306 us  [draw_packet(): long_array = lax.ppermute(u_next, mesh_ax, rows)]
    psum x1 -> x0, waiting for transfers between devices: 170 us -> none  [per_device(): summed = lax.psum(partial_update, 'depth')]
    dot_general x1, matrix products: 94.9 us -> 54.1 us  [per_device(): jnp.einsum('ikar,kjrb->ijab', l_masked, u_masked, precision=HIGH)]
    all_gather x1, waiting for transfers between devices: 27.4 us -> 0.02 us  [per_device(): lax.all_gather(pivot_inv, 'row', axis=1, tiled=True)]
    all_gather x1, waiting for transfers between devices: 26.3 us -> 0.02 us  [per_device(): lax.all_gather(coupling, 'row', axis=1, tiled=True)]
    add x0 -> x1, other arithmetic: none -> 6.45 us  [draw_packet(): u_next = u_next + long_array]
  transfers between devices with their start and end apart: 4 -> 5, of which waited for: 4 -> 3; matrix products, arithmetic and copies ran while one was open for 1% -> 2% of each run, Pallas kernels for 0% -> 0%
where the time goes in v2:
time: 502 us; the launch traced here: 501 us
  waiting for transfers between devices  409 us (81%)
  matrix products  64.9 us (13%)
  between operations  13.2 us (3%)
  other arithmetic  8.49 us (2%)
    ppermute x2, waiting for transfers between devices, draw_packet(): long_array = lax.ppermute(u_next, mesh_ax, rows)  306 us
    all_gather x1, waiting for transfers between devices, per_device(): portion = lax.all_gather(u_cores, 'row', axis=2, tiled=True)  103 us
    dot_general x1, matrix products, per_device(): jnp.einsum('ikar,kjrb->ijab', l_masked, u_masked, precision=HIGH)  54.1 us
  transfers between devices with their start and end apart: 5, of which 3 were waited for; matrix products, arithmetic and copies ran while one was open for 2% of the time, Pallas kernels for 0%

profile of v2, /device:TPU:0, one launch (start us, length us, event | category | flops | bytes accessed | tf_op | source)
XLA Modules:
  0.0 501.3 jit_solution(4868546805948807584)
XLA Ops:
  6.5 0.7 all-gather.4.cloned.1.call-update
  7.3 0.0 all-gather.6.cloned.1.call-start
  7.3 0.1 copy.9
  7.4 0.1 fusion.25
  7.5 0.1 fusion.23
  7.6 103.0 %all-gather.4.cloned.1.call-done = f32[8,4,384,384]{3,2,1,0:T(8,128)} async-done(((f32[8,4,48,384]{3,2,1,0:T(8,128)}), f32[8,4,384,384]{3,2,1,0:T(8,128)}) %all-gather.4.cloned.1.call-update) | async-done | bytes 18874384 | tf_op jit(solution)/shard_map/all_gather | solution.py:40
  110.6 54.1 %fusion.5 = f32[2,4,384,384]{3,2,0,1:T(8,128)} fusion(f32[2,8,384,384]{3,2,1,0:T(8,128)} %param.8, f32[2,8,384]{2,1,0:T(8,128)S(1)} %fusion.25, f32[8,4,384,384]{3,2,1,0:T(8,128)} %all-gather.4.cloned.1.call-done, f32[8,4,384]{2,1,0:T(4,128)S(1)} %fusion.23), kind=kOutput, calls=%fused_computation.6 | convolution fusion | flops 43493621760 | bytes 33103872 | tf_op jit(solution)/shard_map/ikar,kjrb->ijab/dot_general | solution.py:45
  164.7 1.5 collective-permute-start
  166.2 0.0 all-gather.8.cloned.1.call-start
  166.3 102.7 %collective-permute-done = f32[2,4,384,384]{3,2,0,1:T(8,128)} collective-permute-done((f32[2,4,384,384]{3,2,0,1:T(8,128)}, f32[2,4,384,384]{3,2,0,1:T(8,128)}, u32[]{:S(2)}, u32[]{:S(2)}) %collective-permute-start) | collective-permute-done | bytes 4718624 | tf_op jit(solution)/shard_map/ppermute | solution.py:17
  269.0 6.4 %add.9 = f32[2,4,384,384]{3,2,0,1:T(8,128)} add(f32[2,4,384,384]{3,2,0,1:T(8,128)} %fusion.5, f32[2,4,384,384]{3,2,0,1:T(8,128)} %collective-permute-done) | non-fusion elementwise | flops 1179648 | bytes 14155776 | tf_op jit(solution)/shard_map/add | solution.py:18
  275.5 2.4 collective-permute-start.1
  277.9 203.0 %collective-permute-done.1 = f32[2,4,384,384]{3,2,0,1:T(8,128)} collective-permute-done((f32[2,4,384,384]{3,2,0,1:T(8,128)}, f32[2,4,384,384]{3,2,0,1:T(8,128)}, u32[]{:S(2)}, u32[]{:S(2)}) %collective-permute-start.1) | collective-permute-done | bytes 4718624 | tf_op jit(solution)/shard_map/ppermute | solution.py:17
  480.9 1.8 fusion.10
  482.7 0.0 all-gather.6.cloned.1.call-done
  482.7 1.8 fusion.16
  484.6 2.0 fusion.15
  486.6 1.8 fusion.14
  488.4 1.8 fusion.13
  490.2 0.8 fusion.12
  491.0 1.8 fusion.11
  492.8 0.8 convolution_bitcast_fusion
  493.6 0.1 pad_maximum_fusion
  493.7 1.1 copy.12
  (17 shorter events, 0.1 us)
Async XLA Ops:
  6.5 0.8 copy-start.2
  6.5 0.9 copy-start.4
  6.5 0.9 copy-start.3
  6.5 104.1 %all-gather.4.cloned.1.call-start = ((), (), s32[]{:S(2)}) async-start(), calls=%async_computation | async-start | bytes 21233664 | tf_op jit(solution)/shard_map/all_gather | solution.py:40
  7.3 475.5 %all-gather.6.cloned.1.call-start = ((), (), s32[]{:S(2)}) async-start(), calls=%async_computation.1 | async-start | bytes 2654208 | tf_op jit(solution)/shard_map/all_gather | solution.py:31
  164.7 104.3 %collective-permute-start = (f32[2,4,384,384]{3,2,0,1:T(8,128)}, f32[2,4,384,384]{3,2,0,1:T(8,128)}, u32[]{:S(2)}, u32[]{:S(2)}) collective-permute-start(f32[2,4,384,384]{3,2,0,1:T(8,128)} %fusion.5), channel_id=1, source_target_pairs={{0,1},{1,0},{2,3},{3,2},{4,5},{5,4},{6,7},{7,6},{8,9},{9,8},{10,11... | collective-permute-start | bytes 14155784 | tf_op jit(solution)/shard_map/ppermute | solution.py:17
  166.2 314.7 %copy-start.1 = (f32[2,4,96,384]{3,2,1,0:T(8,128)S(1)}, f32[2,4,96,384]{3,2,1,0:T(8,128)}, u32[]{:S(2)}) copy-start(f32[2,4,96,384]{3,2,1,0:T(8,128)} %param.13) | copy-start | bytes 3538948
  166.2 318.3 %all-gather.8.cloned.1.call-start = ((), (), s32[]{:S(2)}) async-start(), calls=%async_computation.2 | async-start | bytes 1990656 | tf_op jit(solution)/shard_map/all_gather | solution.py:32
  275.5 205.4 %collective-permute-start.1 = (f32[2,4,384,384]{3,2,0,1:T(8,128)}, f32[2,4,384,384]{3,2,0,1:T(8,128)}, u32[]{:S(2)}, u32[]{:S(2)}) collective-permute-start(f32[2,4,384,384]{3,2,0,1:T(8,128)} %add.9), channel_id=1, source_target_pairs={{0,2},{1,3},{2,0},{3,1},{4,6},{5,7},{6,4},{7,5},{8,10},{9,11},{10,... | collective-permute-start | bytes 14155784 | tf_op jit(solution)/shard_map/ppermute | solution.py:17
  484.6 5.6 %copy-start = (f32[4,384,384]{2,1,0:T(8,128)S(1)}, f32[4,384,384]{2,1,0:T(8,128)}, u32[]{:S(2)}) copy-start(f32[4,384,384]{2,1,0:T(8,128)} %all-gather.6.cloned.1.call-done) | copy-start | bytes 7077892
Sparse Core Ops, SparseCore 0:
  9.2 101.3 all-gather.3
  166.4 27.9 all-gather.5
  278.0 24.5 all-gather.7
